TPU v7x, 32 devices: a whole 2x2x4 slice. The times are simulated.
32 devices in a mesh: grp: 4 (over y, core), dev: 8 (over z, x).
Axes of the slice: x: 2, y: 2, z: 4, core: 2. Of those that a mesh axis runs over, the one named last changes fastest.
Arguments:
- old_fine: float32 [512, 9, 64, 128], P('dev', None, 'grp'), may hold values from -6 to 6
- old_ids: int32 [4, 512], P('grp', 'dev'), may hold values from -1 to 511, as said below
- old_coarse: float32 [256, 9, 32, 64], P('dev', None, 'grp'), may hold values from -6 to 6
- coarse_ids: int32 [4, 256], P('grp', 'dev'), may hold values from 0 to 255, as said below
- velocity: float32 [512, 3, 64, 128], P('dev', None, 'grp'), may hold values from -0.12 to 0.12
- diffusion: float32 [9], replicated, may hold values from 0.01 to 0.1
Outputs:
- species_out: float32 [512, 9, 64, 128], P('dev', None, 'grp')
Inputs may be any that keep to these rules, and one draw needn't show every extreme that they name: `old_ids`: row g names, for each old fine slot k of group g (on dev index k // 64), the x-plane that the slot holds, or -1 for an empty slot whose rows of old_fine are ignored. No plane is named twice; planes named nowhere are newly refined. The slots of one device hold at most 16 planes of any one new box, box e holding planes e * 64 to e * 64 + 63. `coarse_ids`: each row is a permutation. The slots of one device hold at most 8 of the coarse planes e * 32 to e * 32 + 31 of any one new box e.
All inputs are finite; a program needn't handle non-finite values.
Results may differ from a plain program's by a relative error of at most 0.000092.
Values sent between devices are 32-bit elements; how exact they have to be, the bound alone decides.
A program may use at most 192 MiB of HBM per device.

v0:
```python
import jax
import jax.numpy as jnp
from jax import lax
from jax.sharding import PartitionSpec as P

ITERS = 2


HIGHEST = lax.Precision.HIGHEST


def with_halo(value, sides, width):
    for axis, dim in sides:
        size, length = (lax.axis_size(axis), value.shape[dim])
        up = [(i, (i + 1) % size) for i in range(size - 1)]
        down = [(j, i) for i, j in up]
        last = lax.slice_in_dim(value, length - width, length, axis=dim)
        leading = lax.slice_in_dim(value, 0, width, axis=dim)
        before = lax.ppermute(last, axis, up)
        after = lax.ppermute(leading, axis, down)
        value = jnp.concatenate([before, value, after], axis=dim)
    return value


def refine(coarse):
    extent = coarse.shape
    ypadded = jnp.concatenate([coarse[:, :, :1], coarse, coarse[:, :, -1:]], axis=2)
    zpadded = jnp.concatenate([coarse[..., :1], coarse, coarse[..., -1:]], axis=3)
    slope_y = 0.5 * (ypadded[:, :, 2:] - ypadded[:, :, :-2])
    slope_z = 0.5 * (zpadded[..., 2:] - zpadded[..., :-2])
    row_parts = []
    for row_half in range(2):
        col_parts = [
            coarse + (0.5 * row_half - 0.25) * slope_y + (0.5 * col_half - 0.25) * slope_z
            for col_half in range(2)
        ]
        row_parts.append(jnp.stack(col_parts, axis=-1))
    children = jnp.stack(row_parts, axis=3)
    refined = children.reshape(extent[0], extent[1], 2 * extent[2], 2 * extent[3])
    return jnp.repeat(refined, 2, axis=0)


def advance(padded, flow_field, diffusion):
    center = padded[1:-1, :, 1:-1]
    zpadded = jnp.concatenate([center[..., :1], center, center[..., -1:]], axis=3)
    minus_side = [padded[:-2, :, 1:-1], padded[1:-1, :, :-2], zpadded[..., :-2]]
    plus_side = [padded[2:, :, 1:-1], padded[1:-1, :, 2:], zpadded[..., 2:]]
    laplace = (
        minus_side[0]
        + plus_side[0]
        + minus_side[1]
        + plus_side[1]
        + minus_side[2]
        + plus_side[2]
        - 6.0 * center
    )
    transport = jnp.zeros_like(center)
    for direction in range(3):
        speed_part = flow_field[:, direction : direction + 1]
        transport = (
            transport
            + jnp.maximum(speed_part, 0.0) * (center - minus_side[direction])
            + jnp.minimum(speed_part, 0.0) * (plus_side[direction] - center)
        )
    return center + diffusion[None, :, None, None] * laplace - transport


def pack_slots(blocks, labels, block_len, devices, capacity):
    target = jnp.where(labels >= 0, labels // block_len, -1)
    positions = jnp.arange(labels.shape[0])
    earlier = (target[None, :] == target[:, None]) & (positions[None, :] < positions[:, None])
    ranking = jnp.sum(earlier.astype(jnp.int32), axis=1)
    slot_index = jnp.where(labels >= 0, target * capacity + ranking, -1)
    chosen = slot_index[None, :] == jnp.arange(devices * capacity)[:, None]
    outgoing = jnp.dot(chosen.astype(jnp.float32), blocks, precision=HIGHEST)
    within = jnp.sum(jnp.where(chosen, (labels % block_len)[None, :] + 1, 0), axis=1) - 1
    return (outgoing, within)


def unpack_slots(incoming, within, block_len):
    placing = (within[None, :] == jnp.arange(block_len)[:, None]).astype(jnp.float32)
    return (jnp.dot(placing, incoming, precision=HIGHEST), jnp.sum(placing, axis=1))


def on_device(old_fine, old_ids, old_coarse, coarse_ids, velocity, diffusion):
    dev_count = lax.axis_size("dev")
    plane_count = old_fine.shape[0]
    species = old_fine.shape[1]
    row_count = old_fine.shape[2]
    depth_count = old_fine.shape[3]
    fine_capacity = max(2, 2 * plane_count // dev_count)
    outgoing, within = pack_slots(
        old_fine.reshape(plane_count, -1), old_ids[0], plane_count, dev_count, fine_capacity
    )
    arrived, arrived_labels = (
        lax.all_to_all(outgoing, "dev", split_axis=0, concat_axis=0, tiled=True),
        lax.all_to_all(within, "dev", split_axis=0, concat_axis=0, tiled=True),
    )
    moved_rows, filled = unpack_slots(arrived, arrived_labels, plane_count)
    coarse_count = old_coarse.shape[0]
    coarse_flat = old_coarse.reshape(coarse_count, -1)
    coarse_labels = coarse_ids[0]
    coarse_capacity = max(2, 2 * coarse_count // dev_count)
    coarse_out, coarse_within = pack_slots(
        coarse_flat, coarse_labels, coarse_count, dev_count, coarse_capacity
    )
    coarse_in, coarse_in_labels = (
        lax.all_to_all(coarse_out, "dev", split_axis=0, concat_axis=0, tiled=True),
        lax.all_to_all(coarse_within, "dev", split_axis=0, concat_axis=0, tiled=True),
    )
    parents, coarse_filled = unpack_slots(coarse_in, coarse_in_labels, coarse_count)
    interp = refine(parents.reshape(coarse_count, species, row_count // 2, depth_count // 2))
    moved_rows = moved_rows.reshape(plane_count, species, row_count, depth_count)
    species_state = jnp.where((filled < 0.5)[:, None, None, None], interp, moved_rows)
    for repeat in range(ITERS):
        padded = with_halo(species_state, (("grp", 2), ("dev", 0)), 1)
        species_state = advance(padded, velocity, diffusion)
    return species_state


def solution(mesh):
    in_specs = (
        P("dev", None, "grp", None),
        P("grp", "dev"),
        P("dev", None, "grp", None),
        P("grp", "dev"),
        P("dev", None, "grp", None),
        P(),
    )
    out_specs = P("dev", None, "grp", None)
    return jax.shard_map(
        on_device, mesh=mesh, in_specs=in_specs, out_specs=out_specs, check_vma=False
    )
```

profile of v0, /device:TPU:25, one launch (start us, length us, event | category | flops | bytes accessed | tf_op | source)
XLA Modules:
  0.0 362.4 jit_solution(1614253920150574247)
XLA Ops:
  3.0 5.5 %all-to-all-start.1 = ((s32[8,8,1]{1,2,0:T(1,128)}), s32[8,8,1]{1,2,0:T(1,128)S(1)}, u32[]{:S(2)}, u32[]{:S(2)}) async-start(s32[8,8,1]{1,2,0:T(1,128)} %bitcast.11), calls=%async_computation.1 | async-start | bytes 8192 | tf_op jit(solution)/shard_map/all_to_all | solution.py:109
  13.0 5.4 %all-to-all-start = ((s32[8,16,1]{1,2,0:T(1,128)}), s32[8,16,1]{1,2,0:T(1,128)S(1)}, u32[]{:S(2)}, u32[]{:S(2)}) async-start(s32[8,16,1]{1,2,0:T(1,128)} %bitcast.5), calls=%async_computation | async-start | bytes 8192 | tf_op jit(solution)/shard_map/all_to_all | solution.py:97
  20.8 6.5 %all-to-all-start.2 = ((f32[8,8,4608]{2,1,0:T(8,128)}), f32[8,8,4608]{2,1,0:T(8,128)S(1)}, u32[]{:S(2)}, u32[]{:S(2)}) async-start(f32[8,8,4608]{2,1,0:T(8,128)} %fusion.53), calls=%async_computation.2 | async-start | bytes 2359296 | tf_op jit(solution)/shard_map/all_to_all | solution.py:108
  27.3 5.2 %reshape.168 = f32[64,18432,1]{1,0,2:T(8,128)} reshape(f32[64,9,16,128]{3,2,1,0:T(8,128)} %param.6) | data formatting | bytes 9437184 | tf_op jit(solution)/shard_map/reshape | solution.py:93
  32.5 9.6 %fusion.46 = f32[8,16,18432]{2,1,0:T(8,128)} fusion(f32[64,18432,1]{1,0,2:T(8,128)} %reshape.168, s32[8,16]{1,0:T(8,128)S(1)} %multiply_add_fusion.2, s32[64]{0:T(128)S(1)} %get-tuple-element.31), kind=kOutput, calls=%fused_computation.92 | convolution fusion | flops 1811947520 | bytes 14156544 | tf_op jit(solution)/shard_map/dot_general | solution.py:75
  42.0 10.7 %all-to-all-done.2 = f32[8,8,4608]{2,1,0:T(8,128)S(1)} async-done(((f32[8,8,4608]{2,1,0:T(8,128)}), f32[8,8,4608]{2,1,0:T(8,128)S(1)}, u32[]{:S(2)}, u32[]{:S(2)}) %all-to-all-start.2) | async-done | bytes 1179680 | tf_op jit(solution)/shard_map/all_to_all | solution.py:108
  52.8 6.9 %all-to-all-start.3 = ((f32[8,16,18432]{2,1,0:T(8,128)}), f32[8,16,18432]{2,1,0:T(8,128)}, u32[]{:S(2)}, u32[]{:S(2)}) async-start(f32[8,16,18432]{2,1,0:T(8,128)} %fusion.46), calls=%async_computation.3 | async-start | bytes 18874368 | tf_op jit(solution)/shard_map/all_to_all | solution.py:96
  62.6 3.4 fusion.60
  72.1 12.7 %copy.43 = f32[32,9,8,2,64,2]{0,5,4,3,2,1:T(2,128)} copy(f32[32,9,8,2,64,2]{4,0,2,1,5,3:T(8,128)} %pad_maximum_fusion.20) | data formatting | bytes 4718592 | tf_op jit(solution)/shard_map/stack | solution.py:38
  84.8 6.7 %copy.44 = f32[32,9,16,128]{3,0,2,1:T(8,128)} copy(f32[32,9,16,128]{0,3,2,1:T(8,128)} %bitcast.93) | data formatting | bytes 4718592 | tf_op jit(solution)/shard_map/reshape | solution.py:39
  91.5 173.0 %all-to-all-done.3 = f32[8,16,18432]{2,1,0:T(8,128)} async-done(((f32[8,16,18432]{2,1,0:T(8,128)}), f32[8,16,18432]{2,1,0:T(8,128)}, u32[]{:S(2)}, u32[]{:S(2)}) %all-to-all-start.3) | async-done | bytes 9437216 | tf_op jit(solution)/shard_map/all_to_all | solution.py:96
  264.5 9.6 %copy.45 = f32[18432,128]{1,0:T(8,128)} copy(f32[18432,128]{0,1:T(8,128)} %bitcast.28) | data formatting | bytes 18874368 | tf_op jit(solution)/shard_map/dot_general | solution.py:82
  274.0 3.6 broadcast_in_dim.73
  277.7 8.3 %broadcast_select_fusion = f32[64,9,16,128]{3,0,2,1:T(8,128)S(1)} fusion(f32[64,9,16,128]{3,0,2,1:T(8,128)S(1)} %bitcast.94, pred[64]{0:T(512)(128)(4,1)S(1)} %broadcast_compare_fusion, f32[9,16,128,128]{3,2,1,0:T(8,128)} %bitcast.92, s32[128]{0:T(128)S(1)} %eq.136), kind=kOutput, calls=%fused_computation.67 | convolution fusion | flops 1813127168 | bytes 18874944 | tf_op jit(solution)/shard_map/dot_general | solution.py:82
  286.0 3.5 collective-permute-start
  300.2 3.9 %collective-permute-start.3 = (f32[1,9,18,128]{3,0,2,1:T(1,128)S(1)}, f32[1,9,18,128]{3,0,2,1:T(1,128)S(1)}, u32[]{:S(2)}, u32[]{:S(2)}) collective-permute-start(f32[1,9,18,128]{3,0,2,1:T(1,128)S(1)} %get-tuple-element.8), channel_id=1, source_target_pairs={{1,0},{2,1},{3,2},{4,3},{5,4},{6,5},{7,6},{9,8},{10,9},{11,10},{12... | collective-permute-start | bytes 248840 | tf_op jit(solution)/shard_map/ppermute | solution.py:20
  304.1 4.1 %fusion.71 = (f32[64,9,16,1]{3,0,2,1:T(8,128)S(1)}, f32[64,9,16,1]{3,0,2,1:T(8,128)}) fusion(f32[64,9,16,128]{3,0,2,1:T(8,128)S(1)} %broadcast_select_fusion), kind=kLoop, calls=%fused_computation.159 | loop fusion | bytes 147456 | tf_op jit(solution)/shard_map/slice | solution.py:45
  308.3 13.1 %fusion.28 = f32[64,9,16,128]{3,0,2,1:T(8,128)S(1)} fusion(f32[64,9,16,128]{3,0,2,1:T(8,128)S(1)} %broadcast_select_fusion, f32[64,9,1,128]{3,0,2,1:T(8,128)} %copy-done.1, f32[64,9,1,128]{3,0,2,1:T(8,128)S(1)} %collective-permute-done, f32[1,9,18,128]{3,0,2,1:T(1,128)S(1)} %collective-permute-done.3, f32[1,9,18,128]{3,0,2,1:T(1,128)S(1)} %collective-permute-done.2, ...), kind=kLoop, calls=%fused_computation.41 | loop fusion | flops 43646976 | bytes 13412388 | tf_op jit(solution)/shard_map/sub | solution.py:65
  321.4 4.2 %collective-permute-start.4 = (f32[64,9,1,128]{3,0,2,1:T(8,128)S(1)}, f32[64,9,1,128]{3,0,2,1:T(8,128)S(1)}, u32[]{:S(2)}, u32[]{:S(2)}) collective-permute-start(f32[64,9,1,128]{3,0,2,1:T(8,128)S(1)} %get-tuple-element.11), channel_id=1, source_target_pairs={{0,8},{8,16},{16,24},{1,9},{9,17},{17,25},{2,10},{10,18},{18,26},{... | collective-permute-start | bytes 884744 | tf_op jit(solution)/shard_map/ppermute | solution.py:19
  329.3 4.4 %collective-permute-done.5 = f32[64,9,1,128]{3,0,2,1:T(8,128)S(1)} collective-permute-done((f32[64,9,1,128]{3,0,2,1:T(8,128)S(1)}, f32[64,9,1,128]{3,0,2,1:T(8,128)S(1)}, u32[]{:S(2)}, u32[]{:S(2)}) %collective-permute-start.5) | collective-permute-done | bytes 294944 | tf_op jit(solution)/shard_map/ppermute | solution.py:20
  335.7 4.5 %collective-permute-start.7 = (f32[1,9,18,128]{3,0,2,1:T(1,128)S(1)}, f32[1,9,18,128]{3,0,2,1:T(1,128)S(1)}, u32[]{:S(2)}, u32[]{:S(2)}) collective-permute-start(f32[1,9,18,128]{3,0,2,1:T(1,128)S(1)} %get-tuple-element.6), channel_id=1, source_target_pairs={{1,0},{2,1},{3,2},{4,3},{5,4},{6,5},{7,6},{9,8},{10,9},{11,10},{12... | collective-permute-start | bytes 248840 | tf_op jit(solution)/shard_map/ppermute | solution.py:20
  340.3 4.1 %fusion.69 = (f32[64,9,16,1]{3,0,2,1:T(8,128)S(1)}, f32[64,9,16,1]{3,0,2,1:T(8,128)}) fusion(f32[64,9,16,128]{3,0,2,1:T(8,128)S(1)} %fusion.28), kind=kLoop, calls=%fused_computation.157 | loop fusion | bytes 147456 | tf_op jit(solution)/shard_map/slice | solution.py:45
  344.4 13.1 %fusion.6 = f32[64,9,16,128]{3,0,2,1:T(8,128)S(1)} fusion(f32[64,9,16,128]{3,0,2,1:T(8,128)S(1)} %fusion.28, f32[64,9,1,128]{3,0,2,1:T(8,128)} %copy-done.2, f32[64,9,1,128]{3,0,2,1:T(8,128)S(1)} %collective-permute-done.4, f32[1,9,18,128]{3,0,2,1:T(1,128)S(1)} %collective-permute-done.7, f32[1,9,18,128]{3,0,2,1:T(1,128)S(1)} %collective-permute-done.6, ...), kind=kLoop, calls=%fused_computation.9 | loop fusion | flops 43646976 | bytes 13412388 | tf_op jit(solution)/shard_map/sub | solution.py:65
  357.5 4.9 %copy.52 = f32[64,9,16,128]{3,2,1,0:T(8,128)} copy(f32[64,9,16,128]{3,0,2,1:T(8,128)S(1)} %fusion.6) | data formatting | bytes 9437184 | tf_op jit(solution)/shard_map/sub | solution.py:65
  (64 shorter events, 35.3 us)
Async XLA Ops:
  3.0 10.0 %all-to-all-start.1 = ((s32[8,8,1]{1,2,0:T(1,128)}), s32[8,8,1]{1,2,0:T(1,128)S(1)}, u32[]{:S(2)}, u32[]{:S(2)}) async-start(s32[8,8,1]{1,2,0:T(1,128)} %bitcast.11), calls=%async_computation.1 | async-start | bytes 8192 | tf_op jit(solution)/shard_map/all_to_all | solution.py:109
  13.0 7.8 %all-to-all-start = ((s32[8,16,1]{1,2,0:T(1,128)}), s32[8,16,1]{1,2,0:T(1,128)S(1)}, u32[]{:S(2)}, u32[]{:S(2)}) async-start(s32[8,16,1]{1,2,0:T(1,128)} %bitcast.5), calls=%async_computation | async-start | bytes 8192 | tf_op jit(solution)/shard_map/all_to_all | solution.py:97
  20.8 32.0 %all-to-all-start.2 = ((f32[8,8,4608]{2,1,0:T(8,128)}), f32[8,8,4608]{2,1,0:T(8,128)S(1)}, u32[]{:S(2)}, u32[]{:S(2)}) async-start(f32[8,8,4608]{2,1,0:T(8,128)} %fusion.53), calls=%async_computation.2 | async-start | bytes 2359296 | tf_op jit(solution)/shard_map/all_to_all | solution.py:108
  52.8 211.7 %all-to-all-start.3 = ((f32[8,16,18432]{2,1,0:T(8,128)}), f32[8,16,18432]{2,1,0:T(8,128)}, u32[]{:S(2)}, u32[]{:S(2)}) async-start(f32[8,16,18432]{2,1,0:T(8,128)} %fusion.46), calls=%async_computation.3 | async-start | bytes 18874368 | tf_op jit(solution)/shard_map/all_to_all | solution.py:96
  277.6 14.1 %copy-start = (f32[64,3,16,128]{3,2,1,0:T(8,128)S(1)}, f32[64,3,16,128]{3,2,1,0:T(8,128)}, u32[]{:S(2)}) copy-start(f32[64,3,16,128]{3,2,1,0:T(8,128)} %param.10) | copy-start | bytes 4718596
  286.0 11.8 %collective-permute-start = (f32[64,9,1,128]{3,0,2,1:T(8,128)S(1)}, f32[64,9,1,128]{3,0,2,1:T(8,128)S(1)}, u32[]{:S(2)}, u32[]{:S(2)}) collective-permute-start(f32[64,9,1,128]{3,0,2,1:T(8,128)S(1)} %get-tuple-element.15), channel_id=1, source_target_pairs={{0,8},{8,16},{16,24},{1,9},{9,17},{17,25},{2,10},{10,18},{18,26},{... | collective-permute-start | bytes 884744 | tf_op jit(solution)/shard_map/ppermute | solution.py:19
  289.6 8.2 %collective-permute-start.1 = (f32[64,9,1,128]{3,0,2,1:T(8,128)S(1)}, f32[64,9,1,128]{3,0,2,1:T(8,128)S(1)}, u32[]{:S(2)}, u32[]{:S(2)}) collective-permute-start(f32[64,9,1,128]{3,0,2,1:T(8,128)S(1)} %get-tuple-element.16), channel_id=1, source_target_pairs={{8,0},{16,8},{24,16},{9,1},{17,9},{25,17},{10,2},{18,10},{26,18},{... | collective-permute-start | bytes 884744 | tf_op jit(solution)/shard_map/ppermute | solution.py:20
  297.8 10.4 %copy-start.1 = (f32[64,9,1,128]{3,0,2,1:T(8,128)}, f32[64,9,1,128]{3,0,2,1:T(8,128)S(1)}, u32[]{:S(2)}) copy-start(f32[64,9,1,128]{3,0,2,1:T(8,128)S(1)} %collective-permute-done.1) | copy-start | bytes 884740
  297.9 10.3 %collective-permute-start.2 = (f32[1,9,18,128]{3,0,2,1:T(1,128)S(1)}, f32[1,9,18,128]{3,0,2,1:T(1,128)S(1)}, u32[]{:S(2)}, u32[]{:S(2)}) collective-permute-start(f32[1,9,18,128]{3,0,2,1:T(1,128)S(1)} %get-tuple-element.7), channel_id=1, source_target_pairs={{0,1},{1,2},{2,3},{3,4},{4,5},{5,6},{6,7},{8,9},{9,10},{10,11},{11... | collective-permute-start | bytes 248840 | tf_op jit(solution)/shard_map/ppermute | solution.py:19
  300.2 8.0 %copy-start.3 = (f32[9]{0:T(128)S(1)}, f32[9]{0:T(128)}, u32[]{:S(2)}) copy-start(f32[9]{0:T(128)} %param.11) | copy-start | bytes 112
  300.2 8.0 %collective-permute-start.3 = (f32[1,9,18,128]{3,0,2,1:T(1,128)S(1)}, f32[1,9,18,128]{3,0,2,1:T(1,128)S(1)}, u32[]{:S(2)}, u32[]{:S(2)}) collective-permute-start(f32[1,9,18,128]{3,0,2,1:T(1,128)S(1)} %get-tuple-element.8), channel_id=1, source_target_pairs={{1,0},{2,1},{3,2},{4,3},{5,4},{6,5},{7,6},{9,8},{10,9},{11,10},{12... | collective-permute-start | bytes 248840 | tf_op jit(solution)/shard_map/ppermute | solution.py:20
  321.4 7.9 %collective-permute-start.4 = (f32[64,9,1,128]{3,0,2,1:T(8,128)S(1)}, f32[64,9,1,128]{3,0,2,1:T(8,128)S(1)}, u32[]{:S(2)}, u32[]{:S(2)}) collective-permute-start(f32[64,9,1,128]{3,0,2,1:T(8,128)S(1)} %get-tuple-element.11), channel_id=1, source_target_pairs={{0,8},{8,16},{16,24},{1,9},{9,17},{17,25},{2,10},{10,18},{18,26},{... | collective-permute-start | bytes 884744 | tf_op jit(solution)/shard_map/ppermute | solution.py:19
  325.6 8.0 %collective-permute-start.5 = (f32[64,9,1,128]{3,0,2,1:T(8,128)S(1)}, f32[64,9,1,128]{3,0,2,1:T(8,128)S(1)}, u32[]{:S(2)}, u32[]{:S(2)}) collective-permute-start(f32[64,9,1,128]{3,0,2,1:T(8,128)S(1)} %get-tuple-element.12), channel_id=1, source_target_pairs={{8,0},{16,8},{24,16},{9,1},{17,9},{25,17},{10,2},{18,10},{26,18},{... | collective-permute-start | bytes 884744 | tf_op jit(solution)/shard_map/ppermute | solution.py:20
  333.7 2.1 copy-start.2
  333.8 10.6 %collective-permute-start.6 = (f32[1,9,18,128]{3,0,2,1:T(1,128)S(1)}, f32[1,9,18,128]{3,0,2,1:T(1,128)S(1)}, u32[]{:S(2)}, u32[]{:S(2)}) collective-permute-start(f32[1,9,18,128]{3,0,2,1:T(1,128)S(1)} %get-tuple-element.5), channel_id=1, source_target_pairs={{0,1},{1,2},{2,3},{3,4},{4,5},{5,6},{6,7},{8,9},{9,10},{10,11},{11... | collective-permute-start | bytes 248840 | tf_op jit(solution)/shard_map/ppermute | solution.py:19
  335.7 8.6 %collective-permute-start.7 = (f32[1,9,18,128]{3,0,2,1:T(1,128)S(1)}, f32[1,9,18,128]{3,0,2,1:T(1,128)S(1)}, u32[]{:S(2)}, u32[]{:S(2)}) collective-permute-start(f32[1,9,18,128]{3,0,2,1:T(1,128)S(1)} %get-tuple-element.6), channel_id=1, source_target_pairs={{1,0},{2,1},{3,2},{4,3},{5,4},{6,5},{7,6},{9,8},{10,9},{11,10},{12... | collective-permute-start | bytes 248840 | tf_op jit(solution)/shard_map/ppermute | solution.py:20
where the time goes:
time: 364 us; the launch traced here: 362 us
  waiting for transfers between devices  190 us (52%)
  local copies, waits for them, and re-layouts  61.7 us (17%)
  starting transfers between devices  48.7 us (13%)
  other arithmetic  38.3 us (11%)
  matrix products  22.9 us (6%)
    all_to_all x1, waiting for transfers between devices, on_device(): lax.all_to_all(outgoing, 'dev', split_axis=0, concat_axis=0, tiled=True)  173 us
    sub x2, other arithmetic, advance(): return center + diffusion[None, :, None, None] * laplace - transport  26.2 us
    another operation x1, local copies, waits for them, and re-layouts, refine(): children = jnp.stack(row_parts, axis=3)  12.7 us
    ppermute x4, starting transfers between devices, with_halo(): after = lax.ppermute(leading, axis, down)  12.5 us
    ppermute x4, starting transfers between devices, with_halo(): before = lax.ppermute(last, axis, up)  11.9 us
    dot_general x2, matrix products, unpack_slots(): jnp.dot(placing, incoming, precision=HIGHEST)  11.7 us
    dot_general x2, matrix products, pack_slots(): outgoing = jnp.dot(chosen.astype(jnp.float32), blocks, precision=HIGHEST)  11.3 us
    all_to_all x1, waiting for transfers between devices, on_device(): lax.all_to_all(coarse_out, 'dev', split_axis=0, concat_axis=0, tiled=True)  10.7 us
  transfers between devices with their start and end apart: 12, of which 5 were waited for; matrix products, arithmetic and copies ran while one was open for 19% of the time, Pallas kernels for 0%

commit v1 on v0

v1 whole, which is shorter than its diff:
```python
import functools

import jax
import jax.numpy as jnp
from jax import lax
from jax.experimental import pallas as pl
from jax.experimental.pallas import tpu as pltpu
from jax.sharding import PartitionSpec as P

ITERS = 2
VMEM_LIMIT = 48 * 1024 * 1024


def params(**more):
    return pltpu.CompilerParams(vmem_limit_bytes=VMEM_LIMIT, **more)


def earlier_count(mask):
    count = mask.shape[-1]
    lower = jnp.arange(count)[None, :] < jnp.arange(count)[:, None]
    return jnp.sum((mask[..., None, :] & lower).astype(jnp.int32), axis=-1)


def send_table(labels, block_len, devices, capacity):
    target = jnp.where(labels >= 0, labels // block_len, -1)
    count = labels.shape[0]
    same = target[None, :] == target[:, None]
    lower = jnp.arange(count)[None, :] < jnp.arange(count)[:, None]
    rank = jnp.sum((same & lower).astype(jnp.int32), axis=1)
    slot = jnp.where(labels >= 0, target * capacity + rank, -1)
    hits = slot[None, :] == jnp.arange(devices * capacity)[:, None]
    return jnp.max(jnp.where(hits, jnp.arange(count)[None, :], 0), axis=1)


def receive_table(labels_all, block_len, capacity, me):
    devices, count = labels_all.shape
    within = labels_all - me * block_len
    valid = (within >= 0) & (within < block_len)
    slot = jnp.arange(devices)[:, None] * capacity + earlier_count(valid)
    flat_within = jnp.where(valid, within, -1).reshape(-1)
    hits = flat_within[None, :] == jnp.arange(block_len)[:, None]
    return jnp.max(jnp.where(hits, slot.reshape(-1)[None, :], -1), axis=1)


def pack_fine_kernel(table, source, out, sem):
    def send(i, carry):
        pltpu.make_async_copy(source.at[table[i]], out.at[i], sem).start()
        return carry

    lax.fori_loop(0, out.shape[0], send, 0)
    pltpu.make_async_copy(out, out, sem).wait()


def pack_fine(table, fine):
    return pl.pallas_call(
        pack_fine_kernel,
        out_shape=jax.ShapeDtypeStruct((table.shape[0],) + fine.shape[1:], fine.dtype),
        in_specs=[
            pl.BlockSpec(memory_space=pltpu.SMEM),
            pl.BlockSpec(memory_space=pltpu.VMEM),
        ],
        out_specs=pl.BlockSpec(memory_space=pl.ANY),
        scratch_shapes=[pltpu.SemaphoreType.DMA],
        compiler_params=params(),
        name="pack_fine",
    )(table, fine)


def pack_coarse_kernel(table, source, out):
    half = source.shape[-1]

    def step(i, carry):
        out[i, :, :, 0:half] = source[table[2 * i]]
        out[i, :, :, half : 2 * half] = source[table[2 * i + 1]]
        return carry

    lax.fori_loop(0, out.shape[0], step, 0)


def pack_coarse(table, coarse):
    shape = (table.shape[0] // 2,) + coarse.shape[1:3] + (2 * coarse.shape[3],)
    return pl.pallas_call(
        pack_coarse_kernel,
        out_shape=jax.ShapeDtypeStruct(shape, coarse.dtype),
        in_specs=[
            pl.BlockSpec(memory_space=pltpu.SMEM),
            pl.BlockSpec(memory_space=pltpu.VMEM),
        ],
        out_specs=pl.BlockSpec(memory_space=pltpu.VMEM),
        compiler_params=params(),
        name="pack_coarse",
    )(table, coarse)


def refine_kernel(table, pairs, weights, out):
    species, rows, depth = pairs.shape[1:]
    half = depth // 2
    lane = lax.broadcasted_iota(jnp.int32, (species * rows, depth), 1)
    row = lax.broadcasted_iota(jnp.int32, (species, rows, depth), 1)

    def step(c, carry):
        slot = jnp.maximum(table[c], 0)
        block = pairs[slot // 2].reshape(species * rows, depth)
        odd = slot % 2
        block = jnp.where((lane >= half).astype(jnp.int32) == odd, block, 0.0)
        spread = jnp.dot(
            block, weights[...], precision=lax.Precision.HIGHEST,
            preferred_element_type=jnp.float32,
        )
        plain = spread[:, :depth].reshape(species, rows, depth)
        sloped = spread[:, depth:].reshape(species, rows, depth)
        below = jnp.where(row == 0, plain, pltpu.roll(plain, 1, 1))
        above = jnp.where(row == rows - 1, plain, pltpu.roll(plain, rows - 1, 1))
        slope = 0.125 * (above - below)
        for s in range(species):
            out[c, s, pl.ds(0, rows, 2), :] = sloped[s] - slope[s]
            out[c, s, pl.ds(1, rows, 2), :] = sloped[s] + slope[s]
        return carry

    lax.fori_loop(0, out.shape[0], step, 0)


def spread_weights(half):
    depth = 2 * half
    coarse = jnp.arange(half)[:, None]
    fine = jnp.arange(depth)[None, :]
    centre = (fine // 2 == coarse).astype(jnp.float32)
    up = (jnp.minimum(fine // 2 + 1, half - 1) == coarse).astype(jnp.float32)
    down = (jnp.maximum(fine // 2 - 1, 0) == coarse).astype(jnp.float32)
    side = jnp.where(fine % 2 == 1, 0.125, -0.125)
    both = jnp.concatenate([centre, centre + side * (up - down)], axis=1)
    return jnp.concatenate([both, both], axis=0)


def refine(table, pairs, weights):
    species, rows, depth = pairs.shape[1:]
    return pl.pallas_call(
        refine_kernel,
        out_shape=jax.ShapeDtypeStruct(
            (table.shape[0], species, 2 * rows, depth), pairs.dtype
        ),
        in_specs=[
            pl.BlockSpec(memory_space=pltpu.SMEM),
            pl.BlockSpec(memory_space=pltpu.VMEM),
            pl.BlockSpec(memory_space=pltpu.VMEM),
        ],
        out_specs=pl.BlockSpec(memory_space=pltpu.VMEM),
        compiler_params=params(),
        cost_estimate=pl.CostEstimate(
            flops=40_000_000, bytes_accessed=30_000_000, transcendentals=0
        ),
        name="refine",
    )(table, pairs, weights)


def assemble_kernel(table, arrived, interp, out, low, high, sem):
    planes = out.shape[0]
    rows = out.shape[2]

    def fetch(p, carry):
        slot = table[p]

        @pl.when(slot >= 0)
        def _():
            pltpu.make_async_copy(arrived.at[slot], out.at[p], sem).start()

        @pl.when(slot < 0)
        def _():
            pltpu.make_async_copy(interp.at[p // 2], out.at[p], sem).start()

        return carry

    lax.fori_loop(0, planes, fetch, 0)
    pltpu.make_async_copy(out, out, sem).wait()

    def edges(p, carry):
        low[p] = out[p, :, 0, :]
        high[p] = out[p, :, rows - 1, :]
        return carry

    lax.fori_loop(0, planes, edges, 0)


def assemble(table, arrived, interp):
    planes = table.shape[0]
    species, rows, depth = arrived.shape[1:]
    edge = jax.ShapeDtypeStruct((planes, species, depth), arrived.dtype)
    return pl.pallas_call(
        assemble_kernel,
        out_shape=(
            jax.ShapeDtypeStruct((planes, species, rows, depth), arrived.dtype),
            edge,
            edge,
        ),
        in_specs=[
            pl.BlockSpec(memory_space=pltpu.SMEM),
            pl.BlockSpec(memory_space=pl.ANY),
            pl.BlockSpec(memory_space=pl.ANY),
        ],
        out_specs=(pl.BlockSpec(memory_space=pltpu.VMEM),) * 3,
        scratch_shapes=[pltpu.SemaphoreType.DMA],
        compiler_params=params(),
        name="assemble",
    )(table, arrived, interp)


def advance_kernel(steps, diffusion, u, before, after, first, last, below, above, flow, out, *edges):
    i = pl.program_id(0)
    block, species, rows, depth = u.shape
    row = lax.broadcasted_iota(jnp.int32, (rows, depth), 0)
    lane = lax.broadcasted_iota(jnp.int32, (rows, depth), 1)

    def plane(x, s):
        return u[x, s]

    for x in range(block):
        v = [flow[x, k] for k in range(3)]
        plus = [jnp.maximum(w, 0.0) for w in v]
        minus = [jnp.maximum(-w, 0.0) for w in v]
        rest = 1.0
        for k in range(3):
            rest = rest - plus[k] - minus[k]
        for s in range(species):
            d = diffusion[s]
            c = u[x, s]
            if x > 0:
                lo = u[x - 1, s]
            else:
                lo = jnp.where(i == 0, first[0, s], before[0, s])
            if x < block - 1:
                hi = u[x + 1, s]
            else:
                hi = jnp.where(i == steps - 1, last[0, s], after[0, s])
            ylo = jnp.where(row == 0, below[x, pl.ds(s, 1), :], pltpu.roll(c, 1, 0))
            yhi = jnp.where(row == rows - 1, above[x, pl.ds(s, 1), :], pltpu.roll(c, rows - 1, 0))
            zlo = jnp.where(lane == 0, c, pltpu.roll(c, 1, 1))
            zhi = jnp.where(lane == depth - 1, c, pltpu.roll(c, depth - 1, 1))
            total = (rest - 6.0 * d) * c
            total = total + (plus[0] + d) * lo + (minus[0] + d) * hi
            total = total + (plus[1] + d) * ylo + (minus[1] + d) * yhi
            total = total + (plus[2] + d) * zlo + (minus[2] + d) * zhi
            out[x, s] = total
            if edges:
                edges[0][x, pl.ds(s, 1), :] = total[0:1]
                edges[1][x, pl.ds(s, 1), :] = total[rows - 1 : rows]


def advance(diffusion, u, first, last, below, above, flow, with_edges):
    planes, species, rows, depth = u.shape
    block = 8 if planes % 8 == 0 else 1
    steps = planes // block
    edge_spec = pl.BlockSpec((block, species, depth), lambda i: (i, 0, 0))
    plane_spec = pl.BlockSpec((1, species, rows, depth), lambda i: (0, 0, 0, 0))
    block_spec = pl.BlockSpec((block, species, rows, depth), lambda i: (i, 0, 0, 0))
    shapes = [jax.ShapeDtypeStruct(u.shape, u.dtype)]
    out_specs = [block_spec]
    if with_edges:
        shapes += [jax.ShapeDtypeStruct((planes, species, depth), u.dtype)] * 2
        out_specs += [edge_spec] * 2
    return pl.pallas_call(
        functools.partial(advance_kernel, steps),
        grid=(steps,),
        out_shape=shapes,
        in_specs=[
            pl.BlockSpec(memory_space=pltpu.SMEM),
            block_spec,
            pl.BlockSpec(
                (1, species, rows, depth), lambda i: (jnp.maximum(i * block - 1, 0), 0, 0, 0)
            ),
            pl.BlockSpec(
                (1, species, rows, depth),
                lambda i: (jnp.minimum(i * block + block, planes - 1), 0, 0, 0),
            ),
            plane_spec,
            plane_spec,
            edge_spec,
            edge_spec,
            pl.BlockSpec((block, 3, rows, depth), lambda i: (i, 0, 0, 0)),
        ],
        out_specs=out_specs,
        compiler_params=params(),
        name="advance",
    )(diffusion, u, u, u, first, last, below, above, flow)


def shift_up(value, axis):
    size = lax.axis_size(axis)
    return lax.ppermute(value, axis, [(i, i + 1) for i in range(size - 1)])


def shift_down(value, axis):
    size = lax.axis_size(axis)
    return lax.ppermute(value, axis, [(i + 1, i) for i in range(size - 1)])


def on_device(old_fine, old_ids, old_coarse, coarse_ids, velocity, diffusion):
    devices = lax.axis_size("dev")
    me = lax.axis_index("dev")
    planes = old_fine.shape[0]
    coarse_planes = old_coarse.shape[0]
    capacity = max(2, 2 * planes // devices)
    coarse_capacity = max(2, 2 * coarse_planes // devices)
    both = jnp.concatenate([old_ids[0], coarse_ids[0]])
    both_all = lax.all_gather(both, "dev")
    fine_send = send_table(old_ids[0], planes, devices, capacity)
    coarse_send = send_table(coarse_ids[0], coarse_planes, devices, coarse_capacity)
    coarse_out = pack_coarse(coarse_send, old_coarse)
    coarse_in = lax.all_to_all(coarse_out, "dev", split_axis=0, concat_axis=0, tiled=True)
    fine_out = pack_fine(fine_send, old_fine)
    fine_in = lax.all_to_all(fine_out, "dev", split_axis=0, concat_axis=0, tiled=True)
    fine_table = receive_table(both_all[:, :planes], planes, capacity, me)
    coarse_table = receive_table(both_all[:, planes:], coarse_planes, coarse_capacity, me)
    interp = refine(coarse_table, coarse_in, spread_weights(old_coarse.shape[3]))
    u, low, high = assemble(fine_table, fine_in, interp)
    for repeat in range(ITERS):
        first = shift_up(u[-1:], "dev")
        last = shift_down(u[:1], "dev")
        below = shift_up(high, "grp")
        above = shift_down(low, "grp")
        more = repeat < ITERS - 1
        outs = advance(diffusion, u, first, last, below, above, velocity, more)
        if more:
            u, low, high = outs
        else:
            u = outs[0]
    return u


def solution(mesh):
    in_specs = (
        P("dev", None, "grp", None),
        P("grp", "dev"),
        P("dev", None, "grp", None),
        P("grp", "dev"),
        P("dev", None, "grp", None),
        P(),
    )
    out_specs = P("dev", None, "grp", None)
    return jax.shard_map(
        on_device, mesh=mesh, in_specs=in_specs, out_specs=out_specs, check_vma=False
    )
```

time: 364 us -> 319 us (0.88)
  blocking collectives: 0 us -> 204 us
  waiting for transfers between devices: 190 us -> 23.9 us
  local copies, waits for them, and re-layouts: 61.7 us -> 6.46 us
  Pallas kernels: 0 us -> 39.9 us
  other arithmetic: 38.3 us -> 3.74 us
  matrix products: 22.9 us -> 0 us
  starting transfers between devices: 48.7 us -> 36.3 us
    unnamed x0 -> x1, blocking collectives: none -> 204 us
    all_to_all x3 -> x1, waiting for transfers between devices: 174 us -> 0.01 us  [on_device(): lax.all_to_all(fine_out, 'dev', split_axis=0, concat_axis=0, tiled=True)]
    pallas_call x0 -> x6, Pallas kernels: none -> 39.9 us  [the longest x2 18.2 us: advance(): pl.pallas_call(functools.partial(advance_kernel, steps), grid=(steps,), o...]
    sub x4 -> x0, other arithmetic: 26.2 us -> none  [the longest x2 26.2 us: advance(): return center + diffusion[None, :, None, None] * laplace - transport]
    dot_general x4 -> x0, matrix products: 22.9 us -> none  [the longest x2 11.7 us: unpack_slots(): jnp.dot(placing, incoming, precision=HIGHEST)]
    reshape x3 -> x0, local copies, waits for them, and re-layouts: 13.4 us -> none  [the longest x1 6.67 us: refine(): children.reshape(extent[0], extent[1], 2 * extent[2], 2 * extent[3])]
    another operation x1 -> x0, local copies, waits for them, and re-layouts: 12.7 us -> none  [refine(): children = jnp.stack(row_parts, axis=3)]
    all_to_all x3 -> x1, starting transfers between devices: 17.8 us -> 5.72 us  [on_device(): lax.all_to_all(fine_out, 'dev', split_axis=0, concat_axis=0, tiled=True)]
  transfers between devices with their start and end apart: 12 -> 10, of which waited for: 5 -> 4; matrix products, arithmetic and copies ran while one was open for 19% -> 1% of each run, Pallas kernels for 0% -> 4%
where the time goes in v1:
time: 319 us; the launch traced here: 315 us
  blocking collectives  204 us (64%)
  Pallas kernels  39.9 us (13%)
  starting transfers between devices  36.3 us (11%)
  waiting for transfers between devices  23.9 us (7%)
  local copies, waits for them, and re-layouts  6.46 us (2%)
  other arithmetic  3.74 us (1%)
    unnamed x1, blocking collectives  204 us
    all_to_all x1, waiting for transfers between devices, on_device(): lax.all_to_all(coarse_out, 'dev', split_axis=0, concat_axis=0, tiled=True)  20.1 us
    pallas_call x2, Pallas kernels, advance(): pl.pallas_call(functools.partial(advance_kernel, steps), grid=(steps,), o...  18.2 us
    ppermute x4, starting transfers between devices, shift_up(): return lax.ppermute(value, axis, [(i, i + 1) for i in range(size - 1)])  14 us
    ppermute x4, starting transfers between devices, shift_down(): return lax.ppermute(value, axis, [(i + 1, i) for i in range(size - 1)])  11.2 us
    pallas_call x1, Pallas kernels, refine(): pl.pallas_call(refine_kernel, out_shape=jax.ShapeDtypeStruct((table.shape...  7.41 us
  transfers between devices with their start and end apart: 10, of which 4 were waited for; matrix products, arithmetic and copies ran while one was open for 1% of the time, Pallas kernels for 4%

profile of v1, /device:TPU:25, one launch (start us, length us, event | category | flops | bytes accessed | tf_op | source)
XLA Modules:
  0.0 314.8 jit_solution(5586996324866080878)
XLA Ops:
  2.3 1.3 copy-done.2
  3.6 4.1 %pack_coarse.1 = f32[32,9,8,128]{3,2,1,0:T(8,128)} custom-call(s32[64]{0:T(128)S(1)} %select_reduce_fusion.3.table, f32[32,9,8,64]{3,2,1,0:T(8,128)S(1)} %copy-done.2), custom_call_target="tpu_custom_call" | custom-call | tf_op jit(solution)/shard_map/pack_coarse/pallas_call | solution.py:82
  7.6 5.5 %all-to-all-start.1 = ((f32[32,9,8,128]{3,2,1,0:T(8,128)}), f32[32,9,8,128]{3,2,1,0:T(8,128)S(1)}, u32[]{:S(2)}, u32[]{:S(2)}) async-start(f32[32,9,8,128]{3,2,1,0:T(8,128)} %pack_coarse.1), calls=%async_computation.1 | async-start | bytes 2359296 | tf_op jit(solution)/shard_map/all_to_all | solution.py:308
  13.4 2.3 copy-done.1
  15.8 4.2 %pack_fine.1 = f32[128,9,16,128]{3,2,1,0:T(8,128)} custom-call(s32[128]{0:T(128)S(1)} %select_reduce_fusion.2.table, f32[64,9,16,128]{3,2,1,0:T(8,128)S(1)} %copy-done.1), custom_call_target="tpu_custom_call" | custom-call | tf_op jit(solution)/shard_map/pack_fine/pallas_call | solution.py:55
  20.0 20.1 %all-to-all-done.1.pairs = f32[32,9,8,128]{3,2,1,0:T(8,128)S(1)} async-done(((f32[32,9,8,128]{3,2,1,0:T(8,128)}), f32[32,9,8,128]{3,2,1,0:T(8,128)S(1)}, u32[]{:S(2)}, u32[]{:S(2)}) %all-to-all-start.1) | async-done | bytes 1179680 | tf_op jit(solution)/shard_map/all_to_all | solution.py:308
  40.1 5.7 %all-to-all-start = ((f32[128,9,16,128]{3,2,1,0:T(8,128)}), f32[128,9,16,128]{3,2,1,0:T(8,128)}, u32[]{:S(2)}, u32[]{:S(2)}) async-start(f32[128,9,16,128]{3,2,1,0:T(8,128)} %pack_fine.1), calls=%async_computation | async-start | bytes 18874368 | tf_op jit(solution)/shard_map/all_to_all | solution.py:310
  47.2 203.6 %all-reduce = s32[768]{0:T(1024)S(1)} all-reduce(s32[768]{0:T(1024)S(1)} %add_dynamic-update-slice_fusion), channel_id=2, replica_groups=mesh['grp'=4,'dev'=8] {'dev'}, use_global_device_ids=true, to_apply=%add | all-reduce | flops 768 | bytes 6144
  252.2 7.4 %refine.1.interp = f32[32,9,16,128]{3,2,1,0:T(8,128)S(1)} custom-call(s32[32]{0:T(128)S(1)} %select_reduce_fusion.1.table, f32[32,9,8,128]{3,2,1,0:T(8,128)S(1)} %all-to-all-done.1.pairs, f32[128,256]{1,0:T(8,128)S(1)} %maximum_maximum_fusion.weights), custom_call_target="tpu_custom_call" | custom-call | flops 40000000 | bytes 30000000 | tf_op jit(solution)/shard_map/refine/pallas_call | solution.py:137
  259.7 6.0 %assemble.1 = (f32[64,9,16,128]{3,2,1,0:T(8,128)}, f32[64,9,128]{2,1,0:T(8,128)S(1)}, f32[64,9,128]{2,1,0:T(8,128)S(1)}) custom-call(s32[64]{0:T(128)S(1)} %select_reduce_fusion.table, f32[128,9,16,128]{3,2,1,0:T(8,128)} %all-to-all-done.arrived, f32[32,9,16,128]{3,2,1,0:T(8,128)S(1)} %refine.1.interp), custom_call_target="tpu_custom_call" | custom-call | tf_op jit(solution)/shard_map/assemble/pallas_call | solution.py:188
  265.7 3.5 %collective-permute-start.2 = (f32[64,9,128]{2,1,0:T(8,128)S(1)}, f32[64,9,128]{2,1,0:T(8,128)S(1)}, u32[]{:S(2)}, u32[]{:S(2)}) collective-permute-start(f32[64,9,128]{2,1,0:T(8,128)S(1)} %get-tuple-element.12), channel_id=1, source_target_pairs={{0,8},{8,16},{16,24},{1,9},{9,17},{17,25},{2,10},{10,18},{18,26},{... | collective-permute-start | bytes 884744 | tf_op jit(solution)/shard_map/ppermute | solution.py:288
  269.2 2.3 collective-permute-start.3
  271.5 0.9 fusion.6
  272.4 3.5 %collective-permute-start = (f32[1,9,16,128]{3,2,1,0:T(8,128)S(1)}, f32[1,9,16,128]{3,2,1,0:T(8,128)S(1)}, u32[]{:S(2)}, u32[]{:S(2)}) collective-permute-start(f32[1,9,16,128]{3,2,1,0:T(8,128)S(1)} %get-tuple-element.24), channel_id=1, source_target_pairs={{0,1},{1,2},{2,3},{3,4},{4,5},{5,6},{6,7},{8,9},{9,10},{10,11},{11... | collective-permute-start | bytes 221192 | tf_op jit(solution)/shard_map/ppermute | solution.py:288
  276.0 2.7 collective-permute-start.1
  279.2 1.8 collective-permute-done.1.last
  281.1 9.1 %advance.2 = (f32[64,9,16,128]{3,2,1,0:T(8,128)}, f32[64,9,128]{2,1,0:T(8,128)S(1)}, f32[64,9,128]{2,1,0:T(8,128)S(1)}) custom-call(f32[9]{0:T(128)S(1)} %copy-done.3, f32[64,9,16,128]{3,2,1,0:T(8,128)} %get-tuple-element.11.u.before.after, f32[64,9,16,128]{3,2,1,0:T(8,128)} %get-tuple-element.11.u.before.after, ...), custom_call_target="tpu_custom_call" | custom-call | tf_op jit(solution)/shard_map/advance/pallas_call | solution.py:260
  290.2 5.1 %collective-permute-start.6 = (f32[64,9,128]{2,1,0:T(8,128)S(1)}, f32[64,9,128]{2,1,0:T(8,128)S(1)}, u32[]{:S(2)}, u32[]{:S(2)}) collective-permute-start(f32[64,9,128]{2,1,0:T(8,128)S(1)} %get-tuple-element.15), channel_id=1, source_target_pairs={{0,8},{8,16},{16,24},{1,9},{9,17},{17,25},{2,10},{10,18},{18,26},{... | collective-permute-start | bytes 884744 | tf_op jit(solution)/shard_map/ppermute | solution.py:288
  295.3 1.9 collective-permute-start.7
  297.2 0.9 fusion.5
  298.1 1.9 collective-permute-start.4
  300.1 4.3 %collective-permute-start.5 = (f32[1,9,16,128]{3,2,1,0:T(8,128)S(1)}, f32[1,9,16,128]{3,2,1,0:T(8,128)S(1)}, u32[]{:S(2)}, u32[]{:S(2)}) collective-permute-start(f32[1,9,16,128]{3,2,1,0:T(8,128)S(1)} %get-tuple-element.21), channel_id=1, source_target_pairs={{1,0},{2,1},{3,2},{4,3},{5,4},{6,5},{7,6},{9,8},{10,9},{11,10},{12... | collective-permute-start | bytes 221192 | tf_op jit(solution)/shard_map/ppermute | solution.py:293
  304.3 1.4 collective-permute-done.5.last
  305.8 9.1 %advance.3 = f32[64,9,16,128]{3,2,1,0:T(8,128)} custom-call(f32[9]{0:T(128)S(1)} %copy-done.3, f32[64,9,16,128]{3,2,1,0:T(8,128)} %get-tuple-element.14.u.before.after, f32[64,9,16,128]{3,2,1,0:T(8,128)} %get-tuple-element.14.u.before.after, f32[64,9,16,128]{3,2,1,0:T(8,128)} %get-tuple-element.14.u.before.after, ...), custom_call_target="tpu_custom_call" | custom-call | tf_op jit(solution)/shard_map/advance/pallas_call | solution.py:260
  (55 shorter events, 5.4 us)
Async XLA Ops:
  0.0 13.1 %copy-start.5 = (s32[1,64]{1,0:T(1,128)S(1)}, s32[1,64]{1,0:T(1,128)}, u32[]{:S(2)}) copy-start(s32[1,64]{1,0:T(1,128)} %param.7) | copy-start | bytes 772
  2.3 1.3 copy-start.2
  7.6 32.4 %all-to-all-start.1 = ((f32[32,9,8,128]{3,2,1,0:T(8,128)}), f32[32,9,8,128]{3,2,1,0:T(8,128)S(1)}, u32[]{:S(2)}, u32[]{:S(2)}) async-start(f32[32,9,8,128]{3,2,1,0:T(8,128)} %pack_coarse.1), calls=%async_computation.1 | async-start | bytes 2359296 | tf_op jit(solution)/shard_map/all_to_all | solution.py:308
  13.4 2.3 copy-start.1
  20.0 25.8 %copy-start.6 = (u32[32]{0:T(128)S(1)}, u32[32]{0:T(128)}, u32[]{:S(2)}) copy-start(u32[32]{0:T(128)} %constant.97) | copy-start | bytes 388
  20.0 27.1 %copy-start.4 = (s32[1,32]{1,0:T(1,128)S(1)}, s32[1,32]{1,0:T(1,128)}, u32[]{:S(2)}) copy-start(s32[1,32]{1,0:T(1,128)} %param.9) | copy-start | bytes 388
  40.1 219.6 %all-to-all-start = ((f32[128,9,16,128]{3,2,1,0:T(8,128)}), f32[128,9,16,128]{3,2,1,0:T(8,128)}, u32[]{:S(2)}, u32[]{:S(2)}) async-start(f32[128,9,16,128]{3,2,1,0:T(8,128)} %pack_fine.1), calls=%async_computation | async-start | bytes 18874368 | tf_op jit(solution)/shard_map/all_to_all | solution.py:310
  259.6 21.4 %copy-start.3 = (f32[9]{0:T(128)S(1)}, f32[9]{0:T(128)}, u32[]{:S(2)}) copy-start(f32[9]{0:T(128)} %diffusion.3) | copy-start | bytes 112
  259.7 21.4 %copy-start = (f32[64,3,16,128]{3,2,1,0:T(8,128)S(1)}, f32[64,3,16,128]{3,2,1,0:T(8,128)}, u32[]{:S(2)}) copy-start(f32[64,3,16,128]{3,2,1,0:T(8,128)} %flow.3) | copy-start | bytes 4718596
  265.7 15.4 %collective-permute-start.2 = (f32[64,9,128]{2,1,0:T(8,128)S(1)}, f32[64,9,128]{2,1,0:T(8,128)S(1)}, u32[]{:S(2)}, u32[]{:S(2)}) collective-permute-start(f32[64,9,128]{2,1,0:T(8,128)S(1)} %get-tuple-element.12), channel_id=1, source_target_pairs={{0,8},{8,16},{16,24},{1,9},{9,17},{17,25},{2,10},{10,18},{18,26},{... | collective-permute-start | bytes 884744 | tf_op jit(solution)/shard_map/ppermute | solution.py:288
  269.2 11.9 %collective-permute-start.3 = (f32[64,9,128]{2,1,0:T(8,128)S(1)}, f32[64,9,128]{2,1,0:T(8,128)S(1)}, u32[]{:S(2)}, u32[]{:S(2)}) collective-permute-start(f32[64,9,128]{2,1,0:T(8,128)S(1)} %get-tuple-element.13), channel_id=1, source_target_pairs={{8,0},{16,8},{24,16},{9,1},{17,9},{25,17},{10,2},{18,10},{26,18},{... | collective-permute-start | bytes 884744 | tf_op jit(solution)/shard_map/ppermute | solution.py:293
  272.4 6.8 %collective-permute-start = (f32[1,9,16,128]{3,2,1,0:T(8,128)S(1)}, f32[1,9,16,128]{3,2,1,0:T(8,128)S(1)}, u32[]{:S(2)}, u32[]{:S(2)}) collective-permute-start(f32[1,9,16,128]{3,2,1,0:T(8,128)S(1)} %get-tuple-element.24), channel_id=1, source_target_pairs={{0,1},{1,2},{2,3},{3,4},{4,5},{5,6},{6,7},{8,9},{9,10},{10,11},{11... | collective-permute-start | bytes 221192 | tf_op jit(solution)/shard_map/ppermute | solution.py:288
  276.0 5.1 %collective-permute-start.1 = (f32[1,9,16,128]{3,2,1,0:T(8,128)S(1)}, f32[1,9,16,128]{3,2,1,0:T(8,128)S(1)}, u32[]{:S(2)}, u32[]{:S(2)}) collective-permute-start(f32[1,9,16,128]{3,2,1,0:T(8,128)S(1)} %get-tuple-element.23), channel_id=1, source_target_pairs={{1,0},{2,1},{3,2},{4,3},{5,4},{6,5},{7,6},{9,8},{10,9},{11,10},{12... | collective-permute-start | bytes 221192 | tf_op jit(solution)/shard_map/ppermute | solution.py:293
  290.2 15.5 %collective-permute-start.6 = (f32[64,9,128]{2,1,0:T(8,128)S(1)}, f32[64,9,128]{2,1,0:T(8,128)S(1)}, u32[]{:S(2)}, u32[]{:S(2)}) collective-permute-start(f32[64,9,128]{2,1,0:T(8,128)S(1)} %get-tuple-element.15), channel_id=1, source_target_pairs={{0,8},{8,16},{16,24},{1,9},{9,17},{17,25},{2,10},{10,18},{18,26},{... | collective-permute-start | bytes 884744 | tf_op jit(solution)/shard_map/ppermute | solution.py:288
  295.3 10.5 %collective-permute-start.7 = (f32[64,9,128]{2,1,0:T(8,128)S(1)}, f32[64,9,128]{2,1,0:T(8,128)S(1)}, u32[]{:S(2)}, u32[]{:S(2)}) collective-permute-start(f32[64,9,128]{2,1,0:T(8,128)S(1)} %get-tuple-element.16), channel_id=1, source_target_pairs={{8,0},{16,8},{24,16},{9,1},{17,9},{25,17},{10,2},{18,10},{26,18},{... | collective-permute-start | bytes 884744 | tf_op jit(solution)/shard_map/ppermute | solution.py:293
  298.1 6.2 %collective-permute-start.4 = (f32[1,9,16,128]{3,2,1,0:T(8,128)S(1)}, f32[1,9,16,128]{3,2,1,0:T(8,128)S(1)}, u32[]{:S(2)}, u32[]{:S(2)}) collective-permute-start(f32[1,9,16,128]{3,2,1,0:T(8,128)S(1)} %get-tuple-element.22), channel_id=1, source_target_pairs={{0,1},{1,2},{2,3},{3,4},{4,5},{5,6},{6,7},{8,9},{9,10},{10,11},{11... | collective-permute-start | bytes 221192 | tf_op jit(solution)/shard_map/ppermute | solution.py:288
  300.1 5.7 %collective-permute-start.5 = (f32[1,9,16,128]{3,2,1,0:T(8,128)S(1)}, f32[1,9,16,128]{3,2,1,0:T(8,128)S(1)}, u32[]{:S(2)}, u32[]{:S(2)}) collective-permute-start(f32[1,9,16,128]{3,2,1,0:T(8,128)S(1)} %get-tuple-element.21), channel_id=1, source_target_pairs={{1,0},{2,1},{3,2},{4,3},{5,4},{6,5},{7,6},{9,8},{10,9},{11,10},{12... | collective-permute-start | bytes 221192 | tf_op jit(solution)/shard_map/ppermute | solution.py:293

commit v2 on v1

--- a/solution.py
+++ b/solution.py
@@ -40,6 +40,104 @@
     flat_within = jnp.where(valid, within, -1).reshape(-1)
     hits = flat_within[None, :] == jnp.arange(block_len)[:, None]
     return jnp.max(jnp.where(hits, slot.reshape(-1)[None, :], -1), axis=1)
+
+
+def pair_count(same):
+    count = same.shape[-1]
+    lower = jnp.arange(count)[None, :] < jnp.arange(count)[:, None]
+    return jnp.sum((same & lower).astype(jnp.int32), axis=-1)
+
+
+def exchange_plan(labels, block_len, first_cap, second_cap):
+    devices = labels.shape[0]
+    part = devices // 2
+    owners = jnp.arange(devices)
+    valid = labels >= 0
+    owner = jnp.where(valid, labels // block_len, -1)
+    rank = pair_count(owner[:, None, :] == owner[:, :, None])
+    over = valid & (rank >= first_cap)
+    half = owner // part
+    order = pair_count(over[:, None, :] & (half[:, None, :] == half[:, :, None]))
+    counts = jnp.sum((owner[:, :, None] == owners).astype(jnp.int32), axis=1)
+    spot = jnp.arange(first_cap)
+    free = (spot >= counts[:, :, None]).astype(jnp.int32)
+    by_half = free.reshape(devices, 2, part, first_cap)
+    level = jnp.sum(by_half, axis=2)
+    higher = jnp.sum(jnp.where(spot[None, :] > spot[:, None], level[:, :, None, :], 0), axis=-1)
+    member = jnp.arange(part)
+    beside = jnp.sum(
+        jnp.where((member[None, :] < member[:, None])[:, :, None], by_half[:, :, None], 0), axis=3
+    )
+    at = jnp.where(by_half > 0, higher[:, :, None, :] + beside, -1)
+    at = at.reshape(devices, 1, devices * first_cap)
+    spots = jnp.arange(devices * first_cap)
+    match = (at == order[:, :, None]) & ((spots // first_cap) // part == half[:, :, None])
+    borrowed = jnp.max(jnp.where(match, spots, -1), axis=-1)
+    slot = jnp.where(valid, jnp.where(over, borrowed, owner * first_cap + rank), -1)
+    via = slot // first_cap
+    relayed = over & (via != owner)
+    lane = jnp.where(relayed, via * part + owner % part, -1)
+    within = pair_count(lane[:, None, :] == lane[:, :, None])
+    lanes = jnp.arange(devices * part)
+    per_source = jnp.sum((lane[:, :, None] == lanes).astype(jnp.int32), axis=1)
+    ahead = jnp.sum(
+        jnp.where((owners[None, :] < owners[:, None])[:, :, None], per_source[None], 0), axis=1
+    )
+    mine = lane[:, :, None] == lanes
+    second = within + jnp.sum(jnp.where(mine, ahead[:, None, :], 0), axis=-1)
+    fits = jnp.all(jnp.where(over, borrowed >= 0, True))
+    fits = fits & jnp.all(jnp.sum(per_source, axis=0) <= second_cap)
+    return owner, slot, relayed, second, fits
+
+
+def plan_tables(labels, plan, block_len, first_cap, second_cap, me):
+    owner, slot, relayed, second, _ = plan
+    devices, count = labels.shape
+    part = devices // 2
+    via = slot // first_cap
+    mine = jnp.max(jnp.where(owners_are(me, devices), slot, -1), axis=0)
+    spots = jnp.arange(devices * first_cap)
+    send = jnp.max(jnp.where(mine[None] == spots[:, None], jnp.arange(count)[None], 0), axis=1)
+    arrive = (jnp.arange(devices)[:, None] * first_cap + slot % first_cap).reshape(-1)
+    handed = jnp.where(relayed & (via == me), (owner % part) * second_cap + second, -1)
+    hops = jnp.arange(part * second_cap)
+    relay = jnp.max(
+        jnp.where(handed.reshape(-1)[None] == hops[:, None], arrive[None], 0), axis=1
+    )
+    direct = arrive.reshape(devices, count)
+    indirect = devices * first_cap + (via % part) * second_cap + second
+    where = jnp.where(relayed, indirect, direct).reshape(-1)
+    inside = jnp.where(owner == me, labels - me * block_len, -1).reshape(-1)
+    hits = inside[None] == jnp.arange(block_len)[:, None]
+    return send, relay, jnp.max(jnp.where(hits, where[None], -1), axis=1)
+
+
+def owners_are(me, devices):
+    return (jnp.arange(devices) == me)[:, None]
+
+
+def pack_relay_kernel(table, arrived, out, sem):
+    def fetch(i, carry):
+        pltpu.make_async_copy(arrived.at[table[i]], out.at[i], sem).start()
+        return carry
+
+    lax.fori_loop(0, out.shape[0], fetch, 0)
+    pltpu.make_async_copy(out, out, sem).wait()
+
+
+def pack_relay(table, arrived):
+    return pl.pallas_call(
+        pack_relay_kernel,
+        out_shape=jax.ShapeDtypeStruct((table.shape[0],) + arrived.shape[1:], arrived.dtype),
+        in_specs=[
+            pl.BlockSpec(memory_space=pltpu.SMEM),
+            pl.BlockSpec(memory_space=pl.ANY),
+        ],
+        out_specs=pl.BlockSpec(memory_space=pltpu.VMEM),
+        scratch_shapes=[pltpu.SemaphoreType.DMA],
+        compiler_params=params(),
+        name="pack_relay",
+    )(table, arrived)
 
 
 def pack_fine_kernel(table, source, out, sem):
@@ -153,16 +251,21 @@
     )(table, pairs, weights)
 
 
-def assemble_kernel(table, arrived, interp, out, low, high, sem):
+def assemble_kernel(table, arrived, passed, interp, out, low, high, sem):
+    near = arrived.shape[0]
     planes = out.shape[0]
     rows = out.shape[2]
 
     def fetch(p, carry):
         slot = table[p]
 
-        @pl.when(slot >= 0)
+        @pl.when((slot >= 0) & (slot < near))
         def _():
             pltpu.make_async_copy(arrived.at[slot], out.at[p], sem).start()
+
+        @pl.when(slot >= near)
+        def _():
+            pltpu.make_async_copy(passed.at[slot - near], out.at[p], sem).start()
 
         @pl.when(slot < 0)
         def _():
@@ -181,7 +284,7 @@
     lax.fori_loop(0, planes, edges, 0)
 
 
-def assemble(table, arrived, interp):
+def assemble(table, arrived, passed, interp):
     planes = table.shape[0]
     species, rows, depth = arrived.shape[1:]
     edge = jax.ShapeDtypeStruct((planes, species, depth), arrived.dtype)
@@ -196,12 +299,13 @@
             pl.BlockSpec(memory_space=pltpu.SMEM),
             pl.BlockSpec(memory_space=pl.ANY),
             pl.BlockSpec(memory_space=pl.ANY),
+            pl.BlockSpec(memory_space=pl.ANY),
         ],
         out_specs=(pl.BlockSpec(memory_space=pltpu.VMEM),) * 3,
         scratch_shapes=[pltpu.SemaphoreType.DMA],
         compiler_params=params(),
         name="assemble",
-    )(table, arrived, interp)
+    )(table, arrived, passed, interp)
 
 
 def advance_kernel(steps, diffusion, u, before, after, first, last, below, above, flow, out, *edges):
@@ -301,17 +405,53 @@
     capacity = max(2, 2 * planes // devices)
     coarse_capacity = max(2, 2 * coarse_planes // devices)
     both = jnp.concatenate([old_ids[0], coarse_ids[0]])
-    both_all = lax.all_gather(both, "dev")
-    fine_send = send_table(old_ids[0], planes, devices, capacity)
+    every = lax.all_gather(both, ("grp", "dev"))
+    groups = every.reshape(lax.axis_size("grp"), devices, -1)
+    here = (jnp.arange(groups.shape[0]) == lax.axis_index("grp"))[:, None, None]
+    both_all = jnp.max(jnp.where(here, groups, -1), axis=0)
+    labels = both_all[:, :planes]
     coarse_send = send_table(coarse_ids[0], coarse_planes, devices, coarse_capacity)
+    coarse_table = receive_table(both_all[:, planes:], coarse_planes, coarse_capacity, me)
+    weights = spread_weights(old_coarse.shape[3])
     coarse_out = pack_coarse(coarse_send, old_coarse)
     coarse_in = lax.all_to_all(coarse_out, "dev", split_axis=0, concat_axis=0, tiled=True)
-    fine_out = pack_fine(fine_send, old_fine)
-    fine_in = lax.all_to_all(fine_out, "dev", split_axis=0, concat_axis=0, tiled=True)
-    fine_table = receive_table(both_all[:, :planes], planes, capacity, me)
-    coarse_table = receive_table(both_all[:, planes:], coarse_planes, coarse_capacity, me)
-    interp = refine(coarse_table, coarse_in, spread_weights(old_coarse.shape[3]))
-    u, low, high = assemble(fine_table, fine_in, interp)
+
+    def padded(fine, coarse):
+        send = send_table(old_ids[0], planes, devices, capacity)
+        table = receive_table(labels, planes, capacity, me)
+        arrived = lax.all_to_all(pack_fine(send, fine), "dev", split_axis=0, concat_axis=0, tiled=True)
+        interp = refine(coarse_table, coarse, weights)
+        return assemble(table, arrived, arrived, interp)
+
+    if capacity >= 16 and devices % 2 == 0:
+        first_cap, second_cap = 5 * capacity // 8, capacity // 4
+        plan = functools.partial(
+            exchange_plan, block_len=planes, first_cap=first_cap, second_cap=second_cap
+        )
+        plans = jax.vmap(plan)(groups[:, :, :planes])
+        fits = jnp.all(plans[4])
+        own = [jnp.max(jnp.where(here, value.astype(jnp.int32), -1), axis=0) for value in plans[:4]]
+        own[2] = own[2] > 0
+        send, relay, table = plan_tables(
+            labels, own + [None], planes, first_cap, second_cap, me
+        )
+        part = devices // 2
+        halves = [list(range(part)), list(range(part, devices))]
+
+        def relayed(fine, coarse):
+            arrived = lax.all_to_all(
+                pack_fine(send, fine), "dev", split_axis=0, concat_axis=0, tiled=True
+            )
+            interp = refine(coarse_table, coarse, weights)
+            passed = lax.all_to_all(
+                pack_relay(relay, arrived), "dev", split_axis=0, concat_axis=0,
+                axis_index_groups=halves, tiled=True,
+            )
+            return assemble(table, arrived, passed, interp)
+
+        u, low, high = lax.cond(fits, relayed, padded, old_fine, coarse_in)
+    else:
+        u, low, high = padded(old_fine, coarse_in)
     for repeat in range(ITERS):
         first = shift_up(u[-1:], "dev")
         last = shift_down(u[:1], "dev")

time: 319 us -> 316 us (level)
  blocking collectives: 204 us -> 46.8 us
  waiting for transfers between devices: 23.9 us -> 134 us
  other arithmetic: 3.74 us -> 20.8 us
  Pallas kernels: 39.9 us -> 53 us
  local copies, waits for them, and re-layouts: 6.46 us -> 15.5 us
    unnamed x1, blocking collectives: 204 us -> 46.8 us
    all_to_all x1 -> x2, waiting for transfers between devices: 0.01 us -> 130 us  [the longest x1 125 us: relayed(): lax.all_to_all(pack_fine(send, fine), 'dev', split_axis=0, concat_axis=0,...]
    all_to_all x1, waiting for transfers between devices: 20.1 us -> 0.01 us  [on_device(): lax.all_to_all(coarse_out, 'dev', split_axis=0, concat_axis=0, tiled=True)]
    reduce_sum x0 -> x11, other arithmetic: none -> 6.94 us  [the longest x3 2.46 us: pair_count(): return jnp.sum((same & lower).astype(jnp.int32), axis=-1)]
    pallas_call x1, Pallas kernels: 4.21 us -> 10.7 us  [pack_fine(): pl.pallas_call(pack_fine_kernel, out_shape=jax.ShapeDtypeStruct((table.sh...]
    all_to_all x1 -> x2, starting transfers between devices: 5.72 us -> 9.53 us  [the longest x1 6 us: relayed(): lax.all_to_all(pack_fine(send, fine), 'dev', split_axis=0, concat_axis=0,...]
    reduce_max x0 -> x8, other arithmetic: none -> 3.63 us  [the longest x1 1.3 us: exchange_plan(): borrowed = jnp.max(jnp.where(match, spots, -1), axis=-1)]
  transfers between devices with their start and end apart: 10 -> 11, of which waited for: 4 -> 5; matrix products, arithmetic and copies ran while one was open for 1% -> 7% of each run, Pallas kernels for 4% -> 3%
where the time goes in v2:
time: 316 us; the launch traced here: 309 us
  waiting for transfers between devices  134 us (42%)
  Pallas kernels  53 us (17%)
  blocking collectives  46.8 us (15%)
  starting transfers between devices  38.5 us (12%)
  other arithmetic  20.8 us (7%)
  local copies, waits for them, and re-layouts  15.5 us (5%)
    all_to_all x1, waiting for transfers between devices, relayed(): lax.all_to_all(pack_fine(send, fine), 'dev', split_axis=0, concat_axis=0,...  125 us
    unnamed x1, blocking collectives  46.8 us
    pallas_call x2, Pallas kernels, advance(): pl.pallas_call(functools.partial(advance_kernel, steps), grid=(steps,), o...  18.3 us
    ppermute x4, starting transfers between devices, shift_up(): return lax.ppermute(value, axis, [(i, i + 1) for i in range(size - 1)])  12 us
    ppermute x4, starting transfers between devices, shift_down(): return lax.ppermute(value, axis, [(i + 1, i) for i in range(size - 1)])  11.5 us
    pallas_call x1, Pallas kernels, pack_fine(): pl.pallas_call(pack_fine_kernel, out_shape=jax.ShapeDtypeStruct((table.sh...  10.7 us
    pallas_call x1, Pallas kernels, assemble(): pl.pallas_call(assemble_kernel, out_shape=(jax.ShapeDtypeStruct((planes,...  8.64 us
    pallas_call x1, Pallas kernels, refine(): pl.pallas_call(refine_kernel, out_shape=jax.ShapeDtypeStruct((table.shape...  8.15 us
  transfers between devices with their start and end apart: 11, of which 5 were waited for; matrix products, arithmetic and copies ran while one was open for 7% of the time, Pallas kernels for 3%

profile of v2, /device:TPU:25, one launch (start us, length us, event | category | flops | bytes accessed | tf_op | source)
XLA Modules:
  0.0 309.5 jit_solution(6751721231131929219)
XLA Ops:
  3.6 4.1 %pack_coarse.1 = f32[32,9,8,128]{3,2,1,0:T(8,128)} custom-call(s32[64]{0:T(128)S(1)} %select_reduce_fusion.16.table, f32[32,9,8,64]{3,2,1,0:T(8,128)S(1)} %copy-done.2), custom_call_target="tpu_custom_call" | custom-call | tf_op jit(solution)/shard_map/pack_coarse/pallas_call | solution.py:180
  7.7 5.5 %all-to-all-start.3 = ((f32[32,9,8,128]{3,2,1,0:T(8,128)}), f32[32,9,8,128]{3,2,1,0:T(8,128)S(1)}, u32[]{:S(2)}, u32[]{:S(2)}) async-start(f32[32,9,8,128]{3,2,1,0:T(8,128)} %pack_coarse.1), calls=%async_computation.3 | async-start | bytes 2359296 | tf_op jit(solution)/shard_map/all_to_all | solution.py:417
  13.4 46.8 %all-reduce = s32[3072]{0:T(1024)S(1)} all-reduce(s32[3072]{0:T(1024)S(1)} %add_dynamic-update-slice_fusion), channel_id=2, replica_groups=mesh['grp'=4,'dev'=8] {'grp','dev'}, use_global_device_ids=true, to_apply=%add | all-reduce | flops 3072 | bytes 24576
  81.1 179.8 %conditional.1 = ((f32[64,9,16,128]{3,2,1,0:T(8,128)}, f32[64,9,128]{2,1,0:T(8,128)}, f32[64,9,128]{2,1,0:T(8,128)})) conditional(s32[]{:T(128)} %convert_element_type.64, (s32[]{:T(128)}, s32[8,64]{1,0:T(8,128)S(1)}, s32[1,64]{1,0:T(1,128)S(1)}, f32[64,9,16,128]{3,2,1,0:T(8,128)}, s32[32]{0:T(128)}, /*index=5*/f32[32,9,8,128]{3,2,1,0:T(8,128)S(1)}, ...), branch_computations={%region_18.23_spmd, %region_23.34_spmd} | conditional | flops 40514928 | bytes 84205496 | solution.py:452
  82.7 10.7 %pack_fine.3 = f32[80,9,16,128]{3,2,1,0:T(8,128)S(1)} custom-call(s32[80]{0:T(128)S(1)} %select_reduce_fusion.5.table, f32[64,9,16,128]{3,2,1,0:T(8,128)} %get-tuple-element.263.source), custom_call_target="tpu_custom_call" | custom-call | tf_op jit(solution)/shard_map/cond/branch_1_fun/pack_fine/pallas_call | solution.py:153
  93.4 2.6 copy-done
  96.0 6.0 %all-to-all-start = ((f32[80,9,16,128]{3,2,1,0:T(8,128)}), f32[80,9,16,128]{3,2,1,0:T(8,128)}, u32[]{:S(2)}, u32[]{:S(2)}) async-start(f32[80,9,16,128]{3,2,1,0:T(8,128)} %copy-done), calls=%async_computation | async-start | bytes 11796480 | tf_op jit(solution)/shard_map/cond/branch_1_fun/all_to_all | solution.py:442
  106.0 125.0 %all-to-all-done.arrived = f32[80,9,16,128]{3,2,1,0:T(8,128)} async-done(((f32[80,9,16,128]{3,2,1,0:T(8,128)}), f32[80,9,16,128]{3,2,1,0:T(8,128)}, u32[]{:S(2)}, u32[]{:S(2)}) %all-to-all-start) | async-done | bytes 5898272 | tf_op jit(solution)/shard_map/cond/branch_1_fun/all_to_all | solution.py:442
  231.0 3.2 %pack_relay.1 = f32[16,9,16,128]{3,2,1,0:T(8,128)} custom-call(s32[16]{0:T(128)S(1)} %select_reduce_fusion.6.table, f32[80,9,16,128]{3,2,1,0:T(8,128)} %all-to-all-done.arrived), custom_call_target="tpu_custom_call" | custom-call | tf_op jit(solution)/shard_map/cond/branch_1_fun/pack_relay/pallas_call | solution.py:129
  234.2 3.5 %all-to-all-start.1 = ((f32[16,9,16,128]{3,2,1,0:T(8,128)}), f32[16,9,16,128]{3,2,1,0:T(8,128)S(1)}, u32[]{:S(2)}, u32[]{:S(2)}) async-start(f32[16,9,16,128]{3,2,1,0:T(8,128)} %pack_relay.1), calls=%async_computation.1 | async-start | bytes 2359296 | tf_op jit(solution)/shard_map/cond/branch_1_fun/all_to_all | solution.py:446
  237.8 8.2 %refine.3.interp = f32[32,9,16,128]{3,2,1,0:T(8,128)S(1)} custom-call(s32[32]{0:T(128)S(1)} %copy-done.16, f32[32,9,8,128]{3,2,1,0:T(8,128)} %copy-done.4, f32[128,256]{1,0:T(8,128)} %get-tuple-element.269.weights), custom_call_target="tpu_custom_call" | custom-call | flops 40000000 | bytes 30000000 | tf_op jit(solution)/shard_map/cond/branch_1_fun/refine/pallas_call | solution.py:235
  247.0 5.1 %all-to-all-done.1.passed = f32[16,9,16,128]{3,2,1,0:T(8,128)S(1)} async-done(((f32[16,9,16,128]{3,2,1,0:T(8,128)}), f32[16,9,16,128]{3,2,1,0:T(8,128)S(1)}, u32[]{:S(2)}, u32[]{:S(2)}) %all-to-all-start.1) | async-done | bytes 1179680 | tf_op jit(solution)/shard_map/cond/branch_1_fun/all_to_all | solution.py:446
  252.2 8.6 %assemble.3 = (f32[64,9,16,128]{3,2,1,0:T(8,128)}, f32[64,9,128]{2,1,0:T(8,128)}, f32[64,9,128]{2,1,0:T(8,128)}) custom-call(s32[64]{0:T(128)S(1)} %select_reduce_fusion.3.table, f32[80,9,16,128]{3,2,1,0:T(8,128)} %all-to-all-done.arrived, f32[16,9,16,128]{3,2,1,0:T(8,128)S(1)} %all-to-all-done.1.passed, f32[32,9,16,128]{3,2,1,0:T(8,128)S(1)} %refine.3.interp), custom_call_target="tpu_custom_call" | custom-call | tf_op jit(solution)/shard_map/cond/branch_1_fun/assemble/pallas_call | solution.py:291
  260.8 2.6 collective-permute-start.2
  263.4 1.9 collective-permute-start.3
  266.3 2.8 collective-permute-start
  269.1 3.4 %collective-permute-start.1 = (f32[1,9,16,128]{3,2,1,0:T(8,128)S(1)}, f32[1,9,16,128]{3,2,1,0:T(8,128)S(1)}, u32[]{:S(2)}, u32[]{:S(2)}) collective-permute-start(f32[1,9,16,128]{3,2,1,0:T(8,128)S(1)} %get-tuple-element.326), channel_id=1, source_target_pairs={{1,0},{2,1},{3,2},{4,3},{5,4},{6,5},{7,6},{9,8},{10,9},{11,10},{12... | collective-permute-start | bytes 221192 | tf_op jit(solution)/shard_map/ppermute | solution.py:397
  272.8 1.8 collective-permute-done.1.last
  276.0 9.2 %advance.2 = (f32[64,9,16,128]{3,2,1,0:T(8,128)}, f32[64,9,128]{2,1,0:T(8,128)S(1)}, f32[64,9,128]{2,1,0:T(8,128)S(1)}) custom-call(f32[9]{0:T(128)S(1)} %copy-done.3, f32[64,9,16,128]{3,2,1,0:T(8,128)} %get-tuple-element.276.u.before.after, f32[64,9,16,128]{3,2,1,0:T(8,128)} %get-tuple-element.276.u.before.after, ...), custom_call_target="tpu_custom_call" | custom-call | tf_op jit(solution)/shard_map/advance/pallas_call | solution.py:364
  285.2 4.7 %collective-permute-start.6 = (f32[64,9,128]{2,1,0:T(8,128)S(1)}, f32[64,9,128]{2,1,0:T(8,128)S(1)}, u32[]{:S(2)}, u32[]{:S(2)}) collective-permute-start(f32[64,9,128]{2,1,0:T(8,128)S(1)} %get-tuple-element.280), channel_id=1, source_target_pairs={{0,8},{8,16},{16,24},{1,9},{9,17},{17,25},{2,10},{10,18},{18,26},{... | collective-permute-start | bytes 884744 | tf_op jit(solution)/shard_map/ppermute | solution.py:392
  289.8 1.9 collective-permute-start.7
  292.7 1.9 collective-permute-start.4
  294.6 4.3 %collective-permute-start.5 = (f32[1,9,16,128]{3,2,1,0:T(8,128)S(1)}, f32[1,9,16,128]{3,2,1,0:T(8,128)S(1)}, u32[]{:S(2)}, u32[]{:S(2)}) collective-permute-start(f32[1,9,16,128]{3,2,1,0:T(8,128)S(1)} %get-tuple-element.324), channel_id=1, source_target_pairs={{1,0},{2,1},{3,2},{4,3},{5,4},{6,5},{7,6},{9,8},{10,9},{11,10},{12... | collective-permute-start | bytes 221192 | tf_op jit(solution)/shard_map/ppermute | solution.py:397
  300.3 9.1 %advance.3 = f32[64,9,16,128]{3,2,1,0:T(8,128)} custom-call(f32[9]{0:T(128)S(1)} %copy-done.3, f32[64,9,16,128]{3,2,1,0:T(8,128)} %get-tuple-element.279.u.before.after, f32[64,9,16,128]{3,2,1,0:T(8,128)} %get-tuple-element.279.u.before.after, f32[64,9,16,128]{3,2,1,0:T(8,128)} %get-tuple-element.279.u.before.after, ...), custom_call_target="tpu_custom_call" | custom-call | tf_op jit(solution)/shard_map/advance/pallas_call | solution.py:364
  (146 shorter events, 35.4 us)
Async XLA Ops:
  0.0 13.2 %copy-start.17 = (s32[1,32]{1,0:T(1,128)S(1)}, s32[1,32]{1,0:T(1,128)}, u32[]{:S(2)}) copy-start(s32[1,32]{1,0:T(1,128)} %param.11) | copy-start | bytes 388
  0.0 13.2 %copy-start.18 = (s32[1,64]{1,0:T(1,128)S(1)}, s32[1,64]{1,0:T(1,128)}, u32[]{:S(2)}) copy-start(s32[1,64]{1,0:T(1,128)} %param.9) | copy-start | bytes 772
  7.7 67.4 %all-to-all-start.3 = ((f32[32,9,8,128]{3,2,1,0:T(8,128)}), f32[32,9,8,128]{3,2,1,0:T(8,128)S(1)}, u32[]{:S(2)}, u32[]{:S(2)}) async-start(f32[32,9,8,128]{3,2,1,0:T(8,128)} %pack_coarse.1), calls=%async_computation.3 | async-start | bytes 2359296 | tf_op jit(solution)/shard_map/all_to_all | solution.py:417
  81.1 193.5 %copy-start.3 = (f32[9]{0:T(128)S(1)}, f32[9]{0:T(128)}, u32[]{:S(2)}) copy-start(f32[9]{0:T(128)} %diffusion.3) | copy-start | bytes 112
  81.1 12.3 %copy-start.4 = (f32[32,9,8,128]{3,2,1,0:T(8,128)}, f32[32,9,8,128]{3,2,1,0:T(8,128)S(1)}, u32[]{:S(2)}) copy-start(f32[32,9,8,128]{3,2,1,0:T(8,128)S(1)} %get-tuple-element.268.pairs) | copy-start | bytes 3538948 | tf_op jit(solution)/shard_map/cond
  96.0 6.8 %copy-start.15 = (s32[8,8]{1,0:T(8,128)S(1)}, s32[8,8]{1,0:T(8,128)}, u32[]{:S(2)}) copy-start(s32[8,8]{1,0:T(8,128)} %get-tuple-element.253) | copy-start | bytes 772 | tf_op jit(solution)/shard_map/cond
  96.0 8.5 %copy-start.8 = (s32[4,8,64]{2,1,0:T(8,128)S(1)}, s32[4,8,64]{2,1,0:T(8,128)}, u32[]{:S(2)}) copy-start(s32[4,8,64]{2,1,0:T(8,128)} %copy-done.7) | copy-start | bytes 24580 | tf_op jit(solution)/shard_map/cond
  96.0 8.5 %copy-start.10 = (s32[4,8,64]{2,1,0:T(8,128)S(1)}, s32[4,8,64]{2,1,0:T(8,128)}, u32[]{:S(2)}) copy-start(s32[4,8,64]{2,1,0:T(8,128)} %get-tuple-element.362) | copy-start | bytes 24580 | tf_op jit(solution)/shard_map/cond
  96.0 8.5 %copy-start.11 = (s32[4,8,64]{2,1,0:T(8,128)S(1)}, s32[4,8,64]{2,1,0:T(8,128)}, u32[]{:S(2)}) copy-start(s32[4,8,64]{2,1,0:T(8,128)} %get-tuple-element.246) | copy-start | bytes 24580 | tf_op jit(solution)/shard_map/cond
  96.0 8.5 %copy-start.12 = (pred[4,8,64]{2,1,0:T(8,128)(4,1)S(1)}, pred[4,8,64]{2,1,0:T(8,128)(4,1)}, u32[]{:S(2)}) copy-start(pred[4,8,64]{2,1,0:T(8,128)(4,1)} %get-tuple-element.245) | copy-start | bytes 6148 | tf_op jit(solution)/shard_map/cond
  96.0 9.1 %copy-start.19 = (s32[8]{0:T(128)S(1)}, s32[8]{0:T(128)}, u32[]{:S(2)}) copy-start(s32[8]{0:T(128)} %get-tuple-element.255) | copy-start | bytes 100 | tf_op jit(solution)/shard_map/cond
  96.0 9.2 %copy-start.13 = (s32[1,512]{1,0:T(1,128)S(1)}, s32[1,512]{1,0:T(1,128)}, u32[]{:S(2)}) copy-start(s32[1,512]{1,0:T(1,128)} %get-tuple-element.298) | copy-start | bytes 6148 | tf_op jit(solution)/shard_map/cond
  96.0 9.9 %copy-start.9 = (s32[16,512]{1,0:T(8,128)S(1)}, s32[16,512]{1,0:T(8,128)}, u32[]{:S(2)}) copy-start(s32[16,512]{1,0:T(8,128)} %get-tuple-element.266) | copy-start | bytes 98308 | tf_op jit(solution)/shard_map/cond
  96.0 135.0 %all-to-all-start = ((f32[80,9,16,128]{3,2,1,0:T(8,128)}), f32[80,9,16,128]{3,2,1,0:T(8,128)}, u32[]{:S(2)}, u32[]{:S(2)}) async-start(f32[80,9,16,128]{3,2,1,0:T(8,128)} %copy-done), calls=%async_computation | async-start | bytes 11796480 | tf_op jit(solution)/shard_map/cond/branch_1_fun/all_to_all | solution.py:442
  106.0 131.9 %copy-start.16 = (s32[32]{0:T(128)S(1)}, s32[32]{0:T(128)}, u32[]{:S(2)}) copy-start(s32[32]{0:T(128)} %get-tuple-element.267.table) | copy-start | bytes 388 | tf_op jit(solution)/shard_map/cond
  234.2 18.0 %all-to-all-start.1 = ((f32[16,9,16,128]{3,2,1,0:T(8,128)}), f32[16,9,16,128]{3,2,1,0:T(8,128)S(1)}, u32[]{:S(2)}, u32[]{:S(2)}) async-start(f32[16,9,16,128]{3,2,1,0:T(8,128)} %pack_relay.1), calls=%async_computation.1 | async-start | bytes 2359296 | tf_op jit(solution)/shard_map/cond/branch_1_fun/all_to_all | solution.py:446
  260.8 13.8 %collective-permute-start.2 = (f32[64,9,128]{2,1,0:T(8,128)}, f32[64,9,128]{2,1,0:T(8,128)S(1)}, u32[]{:S(2)}, u32[]{:S(2)}) collective-permute-start(f32[64,9,128]{2,1,0:T(8,128)} %get-tuple-element.277), channel_id=1, source_target_pairs={{0,8},{8,16},{16,24},{1,9},{9,17},{17,25},{2,10},{10,18},{18,26},{... | collective-permute-start | bytes 884744 | tf_op jit(solution)/shard_map/ppermute | solution.py:392
  263.4 11.2 %collective-permute-start.3 = (f32[64,9,128]{2,1,0:T(8,128)}, f32[64,9,128]{2,1,0:T(8,128)S(1)}, u32[]{:S(2)}, u32[]{:S(2)}) collective-permute-start(f32[64,9,128]{2,1,0:T(8,128)} %get-tuple-element.278), channel_id=1, source_target_pairs={{8,0},{16,8},{24,16},{9,1},{17,9},{25,17},{10,2},{18,10},{26,18},{... | collective-permute-start | bytes 884744 | tf_op jit(solution)/shard_map/ppermute | solution.py:397
  266.3 6.5 %collective-permute-start = (f32[1,9,16,128]{3,2,1,0:T(8,128)S(1)}, f32[1,9,16,128]{3,2,1,0:T(8,128)S(1)}, u32[]{:S(2)}, u32[]{:S(2)}) collective-permute-start(f32[1,9,16,128]{3,2,1,0:T(8,128)S(1)} %get-tuple-element.327), channel_id=1, source_target_pairs={{0,1},{1,2},{2,3},{3,4},{4,5},{5,6},{6,7},{8,9},{9,10},{10,11},{11... | collective-permute-start | bytes 221192 | tf_op jit(solution)/shard_map/ppermute | solution.py:392
  269.1 5.5 %collective-permute-start.1 = (f32[1,9,16,128]{3,2,1,0:T(8,128)S(1)}, f32[1,9,16,128]{3,2,1,0:T(8,128)S(1)}, u32[]{:S(2)}, u32[]{:S(2)}) collective-permute-start(f32[1,9,16,128]{3,2,1,0:T(8,128)S(1)} %get-tuple-element.326), channel_id=1, source_target_pairs={{1,0},{2,1},{3,2},{4,3},{5,4},{6,5},{7,6},{9,8},{10,9},{11,10},{12... | collective-permute-start | bytes 221192 | tf_op jit(solution)/shard_map/ppermute | solution.py:397
  285.2 15.1 %collective-permute-start.6 = (f32[64,9,128]{2,1,0:T(8,128)S(1)}, f32[64,9,128]{2,1,0:T(8,128)S(1)}, u32[]{:S(2)}, u32[]{:S(2)}) collective-permute-start(f32[64,9,128]{2,1,0:T(8,128)S(1)} %get-tuple-element.280), channel_id=1, source_target_pairs={{0,8},{8,16},{16,24},{1,9},{9,17},{17,25},{2,10},{10,18},{18,26},{... | collective-permute-start | bytes 884744 | tf_op jit(solution)/shard_map/ppermute | solution.py:392
  289.8 10.5 %collective-permute-start.7 = (f32[64,9,128]{2,1,0:T(8,128)S(1)}, f32[64,9,128]{2,1,0:T(8,128)S(1)}, u32[]{:S(2)}, u32[]{:S(2)}) collective-permute-start(f32[64,9,128]{2,1,0:T(8,128)S(1)} %get-tuple-element.281), channel_id=1, source_target_pairs={{8,0},{16,8},{24,16},{9,1},{17,9},{25,17},{10,2},{18,10},{26,18},{... | collective-permute-start | bytes 884744 | tf_op jit(solution)/shard_map/ppermute | solution.py:397
  292.7 6.2 %collective-permute-start.4 = (f32[1,9,16,128]{3,2,1,0:T(8,128)S(1)}, f32[1,9,16,128]{3,2,1,0:T(8,128)S(1)}, u32[]{:S(2)}, u32[]{:S(2)}) collective-permute-start(f32[1,9,16,128]{3,2,1,0:T(8,128)S(1)} %get-tuple-element.325), channel_id=1, source_target_pairs={{0,1},{1,2},{2,3},{3,4},{4,5},{5,6},{6,7},{8,9},{9,10},{10,11},{11... | collective-permute-start | bytes 221192 | tf_op jit(solution)/shard_map/ppermute | solution.py:392
  294.6 5.7 %collective-permute-start.5 = (f32[1,9,16,128]{3,2,1,0:T(8,128)S(1)}, f32[1,9,16,128]{3,2,1,0:T(8,128)S(1)}, u32[]{:S(2)}, u32[]{:S(2)}) collective-permute-start(f32[1,9,16,128]{3,2,1,0:T(8,128)S(1)} %get-tuple-element.324), channel_id=1, source_target_pairs={{1,0},{2,1},{3,2},{4,3},{5,4},{6,5},{7,6},{9,8},{10,9},{11,10},{12... | collective-permute-start | bytes 221192 | tf_op jit(solution)/shard_map/ppermute | solution.py:397
  (7 other events, 26.0 us)
